TPU v7x, 32 devices: a whole 2x2x4 slice. The times are simulated.
32 devices in a mesh: row: 4 (over x, core), col: 8 (over z, y).
Axes of the slice: x: 2, y: 2, z: 4, core: 2. Of those that a mesh axis runs over, the one named last changes fastest.
Arguments:
- tiles: int32 [4, 8, 8, 128, 128], P('row', 'col'), may hold values from 0 to 1073741823, as said below
- slots: int32 [4, 8, 8], P('row', 'col'), may hold values from 0 to 31, as said below
- factor: float32 [4096, 256], P(('row', 'col')), may hold values from -0.5 to 0.5
- dual: float32 [4096, 256], P(('row', 'col')), may hold values from -0.5 to 0.5
Outputs:
- final_factor: float32 [4096, 256], P(('row', 'col'))
- final_dual: float32 [4096, 256], P(('row', 'col'))
- objective: float32 [3], replicated
- residual: float32 [3], replicated
Inputs may be any that keep to these rules, and one draw needn't show every extreme that they name: `slots`: for every device, 8 distinct block numbers in ascending order. The stored blocks of all devices form a symmetric pattern: the block of rows piece p and columns piece q is stored if and only if the block of rows piece q and columns piece p is; every diagonal block is stored. `tiles`: the stored block of rows piece p and columns piece q is the transpose of the one of rows piece q and columns piece p; diagonal blocks are symmetric.
All inputs are finite; a program needn't handle non-finite values.
Results may differ from a plain program's by a relative error of at most 0.005.
Values may be sent and summed in bfloat16 or wider, within the bound.
A program may use at most 64 MiB of HBM per device.

v0:
```python
import math

import jax
import jax.numpy as jnp
from jax import lax
from jax.sharding import PartitionSpec as P

ITERS = 3


penalty = 2.0
step_size = 0.25
ridge_shift = 0.1
offset = 536870912


def block_weights(integers, vertices):
    unit_scale = math.sqrt(6.0 / vertices) / 2.0**29
    return ((integers - offset).astype(jnp.float32) * unit_scale).astype(jnp.bfloat16)


def unit_rows(values):
    return values * lax.rsqrt(jnp.sum(values * values, axis=1, keepdims=True) + 1e-06)


def local(tiles, slots, factor, dual):
    row_count = lax.axis_size("row")
    col_count = lax.axis_size("col")
    piece_rows = factor.shape[0]
    columns = factor.shape[1]
    vertices = piece_rows * row_count * col_count
    weights = block_weights(tiles.reshape(tiles.shape[2], piece_rows, piece_rows), vertices)
    stored = slots.reshape(-1)
    block_row = stored // row_count
    block_col = stored % row_count

    def combine(partial_value):
        return lax.psum_scatter(partial_value, "col", scatter_dimension=0, tiled=True)

    selector = (block_row[None, :] == jnp.arange(col_count, dtype=jnp.int32)[:, None]).astype(
        jnp.float32
    )
    block_sums = jnp.sum(weights, axis=2, dtype=jnp.float32)
    edge_sums = jnp.dot(selector, block_sums, precision=lax.Precision.HIGHEST)
    degree = combine(edge_sums.reshape(-1))
    current = factor
    lagrange = dual
    projected = unit_rows(current + lagrange / penalty)
    tallies = []
    for iteration in range(ITERS):
        packed = current.astype(jnp.bfloat16)
        own_gram = lax.dot_general(
            packed, packed, (((0,), (0,)), ((), ())), preferred_element_type=jnp.float32
        )
        gram_total = lax.psum(own_gram, ("row", "col"))
        gathered = lax.all_gather(packed, "row", axis=0, tiled=True).reshape(
            -1, piece_rows, columns
        )
        chosen = gathered[block_col]
        products = jnp.einsum("tij,tjk->tik", weights, chosen, preferred_element_type=jnp.float32)
        partial_value = jnp.einsum(
            "at,tik->aik", selector, products, precision=lax.Precision.HIGHEST
        )
        coupled = combine(partial_value.reshape(col_count * piece_rows, columns))
        widened = packed.astype(jnp.float32)
        gradient = degree[:, None] * widened - coupled
        precond = columns / vertices * gram_total + ridge_shift * jnp.eye(
            columns, dtype=jnp.float32
        )
        triangle = jnp.linalg.cholesky(precond)
        descent = 2.0 * gradient - lagrange - penalty * (current - projected)
        current = current + step_size * jax.scipy.linalg.cho_solve((triangle, True), descent.T).T
        projected = unit_rows(current + lagrange / penalty)
        lagrange = lagrange + penalty * (current - projected)
        mismatch = current - projected
        local_sums = jnp.stack([jnp.sum(widened * gradient), jnp.sum(mismatch * mismatch)])
        tallies.append(local_sums)
    stacked = jnp.stack(tallies)
    stacked = lax.psum(stacked, ("row", "col"))
    objective = stacked[:, 0] / (4.0 * vertices)
    residual = stacked[:, 1] / vertices
    return (current, lagrange, objective, residual)


def solution(mesh):
    in_specs = (
        P("row", "col", None, None, None),
        P("row", "col", None),
        P(("row", "col"), None),
        P(("row", "col"), None),
    )
    out_specs = (P(("row", "col"), None), P(("row", "col"), None), P(), P())
    return jax.shard_map(local, mesh=mesh, in_specs=in_specs, out_specs=out_specs, check_vma=False)
```

profile of v0, /device:TPU:0, one launch (start us, length us, event | category | flops | bytes accessed | tf_op | source)
XLA Modules:
  0.0 669.2 jit_solution(12461409791366380685)
XLA Ops:
  10.2 7.2 %all_gather.9 = bf16[512,256]{0,1:T(8,128)(2,1)S(1)} all-gather(bf16[128,256]{0,1:T(8,128)(2,1)S(1)} %get-tuple-element.92), channel_id=1, replica_groups=mesh['row'=4,'col'=8] {'row'}, dimensions={0}, use_global_device_ids=true | all-gather | bytes 327680 | tf_op jit(solution)/shard_map/all_gather | solution.py:56
  21.8 22.3 %all-reduce.1 = f32[1024]{0:T(1024)S(1)} all-reduce(f32[1024]{0:T(1024)S(1)} %convolution_bitcast_fusion), channel_id=2, replica_groups=mesh['row'=4,'col'=8] {'col'}, use_global_device_ids=true, to_apply=%region_6.8.clone | all-reduce | flops 1024 | bytes 8192
  46.1 99.0 %all-reduce.6.cloned.1.call-done = f32[256,256]{0,1:T(8,128)} async-done(((f32[256,256]{0,1:T(8,128)}), f32[256,256]{0,1:T(8,128)}) %all-reduce.6.cloned.1.call-update) | async-done | bytes 262160 | tf_op jit(solution)/shard_map/psum | solution.py:55
  147.1 11.7 %cholesky.172 = f32[128,128]{1,0:T(8,128)S(1)} custom-call(f32[128,128]{1,0:T(8,128)S(1)} %cholesky.270), custom_call_target="Cholesky" | custom-call | tf_op jit(solution)/shard_map/jit(cholesky)/cholesky | solution.py:70
  158.9 9.8 %custom-call.17 = f32[1,128,128]{1,2,0:T(8,128)S(1)} custom-call(f32[1,128,128]{2,1,0:T(8,128)S(1)} %get-tuple-element.104), custom_call_target="InvertDiagBlocksLowerTriangular" | custom-call | tf_op jit(solution)/shard_map/jit(cholesky)/cholesky | solution.py:70
  169.2 11.7 %cholesky.189 = f32[128,128]{1,0:T(8,128)S(1)} custom-call(f32[128,128]{1,0:T(8,128)S(1)} %convolution_subtract_fusion.8), custom_call_target="Cholesky" | custom-call | tf_op jit(solution)/shard_map/jit(cholesky)/cholesky | solution.py:70
  183.0 4.2 while.6
  183.8 1.4 bitcast_dynamic-update-slice_fusion.6
  185.8 1.4 bitcast_dynamic-update-slice_fusion.6
  187.2 19.7 %custom-call.18 = f32[2,128,128]{1,2,0:T(8,128)S(1)} custom-call(f32[2,128,128]{2,1,0:T(8,128)S(1)} %get-tuple-element.26), custom_call_target="InvertDiagBlocksLowerTriangular" | custom-call | tf_op jit(solution)/shard_map/jit(_cho_solve)/triangular_solve | solution.py:72
  209.4 5.8 all_gather.10
  220.1 126.6 %all-reduce.8.cloned.1.call-done = f32[256,256]{0,1:T(8,128)} async-done(((f32[256,256]{0,1:T(8,128)}), f32[256,256]{0,1:T(8,128)}) %all-reduce.8.cloned.1.call-update) | async-done | bytes 262160 | tf_op jit(solution)/shard_map/psum | solution.py:55
  348.7 11.7 %cholesky.206 = f32[128,128]{1,0:T(8,128)S(1)} custom-call(f32[128,128]{1,0:T(8,128)S(1)} %cholesky.273), custom_call_target="Cholesky" | custom-call | tf_op jit(solution)/shard_map/jit(cholesky)/cholesky | solution.py:70
  360.4 9.8 %custom-call.19 = f32[1,128,128]{1,2,0:T(8,128)S(1)} custom-call(f32[1,128,128]{2,1,0:T(8,128)S(1)} %get-tuple-element.100), custom_call_target="InvertDiagBlocksLowerTriangular" | custom-call | tf_op jit(solution)/shard_map/jit(cholesky)/cholesky | solution.py:70
  370.7 11.7 %cholesky.223 = f32[128,128]{1,0:T(8,128)S(1)} custom-call(f32[128,128]{1,0:T(8,128)S(1)} %convolution_subtract_fusion.5), custom_call_target="Cholesky" | custom-call | tf_op jit(solution)/shard_map/jit(cholesky)/cholesky | solution.py:70
  385.1 4.2 while.7
  385.9 1.4 bitcast_dynamic-update-slice_fusion.7
  387.9 1.4 bitcast_dynamic-update-slice_fusion.7
  389.3 19.7 %custom-call.20 = f32[2,128,128]{1,2,0:T(8,128)S(1)} custom-call(f32[2,128,128]{2,1,0:T(8,128)S(1)} %get-tuple-element.27), custom_call_target="InvertDiagBlocksLowerTriangular" | custom-call | tf_op jit(solution)/shard_map/jit(_cho_solve)/triangular_solve | solution.py:72
  409.1 1.6 subtract_bitcast_fusion.1
  413.1 5.8 all_gather.11
  422.7 126.8 %all-reduce.10.cloned.1.call-done = f32[256,256]{0,1:T(8,128)} async-done(((f32[256,256]{0,1:T(8,128)}), f32[256,256]{0,1:T(8,128)}) %all-reduce.10.cloned.1.call-update) | async-done | bytes 262160 | tf_op jit(solution)/shard_map/psum | solution.py:55
  551.5 11.7 %cholesky.240 = f32[128,128]{1,0:T(8,128)S(1)} custom-call(f32[128,128]{1,0:T(8,128)S(1)} %cholesky.276), custom_call_target="Cholesky" | custom-call | tf_op jit(solution)/shard_map/jit(cholesky)/cholesky | solution.py:70
  563.3 9.8 %custom-call.21 = f32[1,128,128]{1,2,0:T(8,128)S(1)} custom-call(f32[1,128,128]{2,1,0:T(8,128)S(1)} %get-tuple-element.96), custom_call_target="InvertDiagBlocksLowerTriangular" | custom-call | tf_op jit(solution)/shard_map/jit(cholesky)/cholesky | solution.py:70
  573.6 11.7 %cholesky.257 = f32[128,128]{1,0:T(8,128)S(1)} custom-call(f32[128,128]{1,0:T(8,128)S(1)} %convolution_subtract_fusion.2), custom_call_target="Cholesky" | custom-call | tf_op jit(solution)/shard_map/jit(cholesky)/cholesky | solution.py:70
  588.0 4.3 while.8
  588.9 1.4 bitcast_dynamic-update-slice_fusion.8
  590.9 1.4 bitcast_dynamic-update-slice_fusion.8
  592.3 19.7 %custom-call.22 = f32[2,128,128]{1,2,0:T(8,128)S(1)} custom-call(f32[2,128,128]{2,1,0:T(8,128)S(1)} %get-tuple-element.28), custom_call_target="InvertDiagBlocksLowerTriangular" | custom-call | tf_op jit(solution)/shard_map/jit(_cho_solve)/triangular_solve | solution.py:72
  612.0 1.7 fusion.7
  619.4 1.4 maximum_bitcast_fusion
  621.5 39.2 %psum.31 = f32[3,2]{1,0:T(4,128)S(1)} all-reduce(f32[3,2]{1,0:T(4,128)S(1)} %pad_maximum_fusion), channel_id=1, replica_groups=mesh['row'=4,'col'=8] {'row','col'}, use_global_device_ids=true, to_apply=%region_22.25 | all-reduce | flops 6 | bytes 48 | tf_op jit(solution)/shard_map/psum | solution.py:79
  (151 shorter events, 42.9 us)
Async XLA Ops:
  8.0 1.1 copy-start.6
  8.0 137.1 %all-reduce.6.cloned.1.call-start = ((), (), s32[]{:S(2)}) async-start(), calls=%async_computation.3 | async-start | bytes 524288 | tf_op jit(solution)/shard_map/psum | solution.py:55
  9.2 8.3 %copy-start.4 = (s32[1,1,8,128,128]{4,3,2,1,0:T(8,128)S(1)}, s32[1,1,8,128,128]{4,3,2,1,0:T(8,128)}, u32[]{:S(2)}) copy-start(s32[1,1,8,128,128]{4,3,2,1,0:T(8,128)} %param.7) | copy-start | bytes 1572868
  10.2 7.3 %copy-start.7 = (s32[1,1,8]{2,1,0:T(1,128)S(1)}, s32[1,1,8]{2,1,0:T(1,128)}, u32[]{:S(2)}) copy-start(s32[1,1,8]{2,1,0:T(1,128)} %param.8) | copy-start | bytes 100
  10.2 196.7 %reduce-scatter.4.cloned.1.call-start = ((), (), s32[]{:S(2)}) async-start(), calls=%async_computation.4 | async-start | bytes 1179648 | tf_op jit(solution)/shard_map/reduce_scatter | solution.py:38
  21.6 325.0 %all-reduce.8.cloned.1.call-start = ((), (), s32[]{:S(2)}) async-start(), calls=%async_computation.5 | async-start | bytes 524288 | tf_op jit(solution)/shard_map/psum | solution.py:55
  44.1 0.7 copy-start.8
  146.1 1.0 copy-start
  219.4 189.6 %reduce-scatter.6.cloned.1.call-start = ((), (), s32[]{:S(2)}) async-start(), calls=%async_computation.6 | async-start | bytes 1179648 | tf_op jit(solution)/shard_map/reduce_scatter | solution.py:38
  220.0 329.5 %all-reduce.10.cloned.1.call-start = ((), (), s32[]{:S(2)}) async-start(), calls=%async_computation.7 | async-start | bytes 524288 | tf_op jit(solution)/shard_map/psum | solution.py:55
  347.6 1.0 copy-start.1
  422.2 189.8 %reduce-scatter.8.cloned.1.call-start = ((), (), s32[]{:S(2)}) async-start(), calls=%async_computation.8 | async-start | bytes 1179648 | tf_op jit(solution)/shard_map/reduce_scatter | solution.py:38
  550.5 1.0 copy-start.2
  587.9 24.1 %copy-start.5 = (f32[128,256]{0,1:T(8,128)S(1)}, f32[128,256]{0,1:T(8,128)}, u32[]{:S(2)}) copy-start(f32[128,256]{0,1:T(8,128)} %reduce-scatter.4.cloned.1.call-done) | copy-start | bytes 393220
  588.0 24.0 %copy-start.3 = (f32[128,256]{0,1:T(8,128)S(1)}, f32[128,256]{0,1:T(8,128)}, u32[]{:S(2)}) copy-start(f32[128,256]{0,1:T(8,128)} %reduce-scatter.6.cloned.1.call-done) | copy-start | bytes 393220
Sparse Core Ops, SparseCore 0:
  14.3 130.7 all-reduce.5
  219.5 127.0 all-reduce.7
  422.3 127.1 all-reduce.9
Sparse Core Ops, SparseCore 1:
  21.7 66.1 reduce-scatter.3
  223.3 63.7 reduce-scatter.5
  426.0 63.8 reduce-scatter.7
where the time goes:
time: 673 us; the launch traced here: 669 us
  waiting for transfers between devices  354 us (53%)
  other arithmetic  176 us (26%)
  blocking collectives  80.4 us (12%)
  local copies, waits for them, and re-layouts  25.8 us (4%)
  between operations  21.1 us (3%)
  matrix products  11.9 us (2%)
    psum x3, waiting for transfers between devices, local(): gram_total = lax.psum(own_gram, ('row', 'col'))  352 us
    another operation x20, other arithmetic, local(): triangle = jnp.linalg.cholesky(precond)  103 us
    another operation x7, other arithmetic, local(): jax.scipy.linalg.cho_solve((triangle, True), descent.T)  59.1 us
    psum x1, blocking collectives, local(): stacked = lax.psum(stacked, ('row', 'col'))  39.2 us
    unnamed x1, blocking collectives  22.3 us
    all_gather x3, blocking collectives, local(): lax.all_gather(packed, 'row', axis=0, tiled=True)  18.8 us
  transfers between devices with their start and end apart: 6, of which 3 were waited for; matrix products, arithmetic and copies ran while one was open for 27% of the time, Pallas kernels for 0%

commit v1 on v0

v1 whole, which is shorter than its diff:
```python
import functools
import math

import jax
import jax.numpy as jnp
from jax import lax
from jax.experimental import pallas as pl
from jax.experimental.pallas import tpu as pltpu
from jax.sharding import PartitionSpec as P

ITERS = 3

penalty = 2.0
step_size = 0.25
ridge_shift = 0.1
offset = 536870912

MESH = pl.DeviceIdType.MESH
VMEM = pltpu.VMEM
HIGHEST = lax.Precision.HIGHEST
F32 = jnp.float32


def block_weights(integers, vertices):
    unit_scale = math.sqrt(6.0 / vertices) / 2.0**29
    return ((integers - offset).astype(jnp.float32) * unit_scale).astype(jnp.bfloat16)


def unit_rows(values):
    return values * lax.rsqrt(jnp.sum(values * values, axis=1, keepdims=True) + 1e-06)


def spread(dims, cols, whole, src, buf, send_sem, recv_sem, use):
    nx, nz, ny = dims
    row, col = lax.axis_index("row"), lax.axis_index("col")
    x, core = row // 2, row % 2
    if whole:
        z, y = col // ny, col % ny
    else:
        z = y = 0

    def device(xx, kk, zz, yy):
        return {"row": xx * 2 + kk, "col": zz * ny + yy if whole else col}

    def piece_of(xx, kk, zz, yy):
        return (xx * 2 + kk) * cols + zz * ny + yy

    barrier = pltpu.get_barrier_semaphore()
    mates = [device(x, core, (z + d) % nz, y) for d in range(1, nz)]
    mates += [device(x, core, z, (y + d) % ny) for d in range(1, ny)]
    mates += [device((x + d) % nx, core, z, y) for d in range(1, nx)]
    mates += [device(x, 1 - core, z, y)]
    for mate in mates:
        pl.semaphore_signal(barrier, inc=1, device_id=mate, device_id_type=MESH)
    pl.semaphore_wait(barrier, len(mates))

    def copy(ref, piece, number, mate):
        return pltpu.make_async_remote_copy(
            src_ref=ref,
            dst_ref=buf.at[piece],
            send_sem=send_sem.at[number],
            recv_sem=recv_sem.at[piece],
            device_id=mate,
            device_id_type=MESH,
        )

    me = piece_of(x, core, z, y)
    for number, mate in enumerate(mates):
        copy(src, me, number, mate).start()
    use(me, src)

    def place(m, kk):
        return piece_of((x + m // (nz * ny)) % nx, kk, (z + m % nz) % nz, (y + m // nz % ny) % ny)

    def arrive(piece):
        copy(src, piece, 0, mates[-1]).wait_recv()

    def stage(first, last, base, onward):
        def body(m, carry):
            piece = place(m, core)
            arrive(piece)
            for d, mate in enumerate(onward):
                copy(buf.at[piece], piece, base + (m - first) * len(onward) + d, mate).start()
            use(piece, buf.at[piece])
            other = place(m - 1, 1 - core)
            arrive(other)
            use(other, buf.at[other])
            return carry

        if last > first:
            lax.fori_loop(first, last, body, 0)
        return base + (last - first) * len(onward)

    base = len(mates)
    base = stage(1, nz, base, mates[nz - 1 :])
    base = stage(nz, nz * ny, base, mates[nz + ny - 2 :])
    base = stage(nz * ny, nz * ny * nx, base, mates[-1:])
    other = place(nz * ny * nx - 1, 1 - core)
    arrive(other)
    use(other, buf.at[other])

    def drain(number, carry):
        copy(src, me, number, mates[-1]).wait_send()
        return carry

    lax.fori_loop(0, base, drain, 0)


def gather_kernel(dims, cols, packed, blocks, gram, coupled, buf, send_sem, recv_sem):
    gram[...] = jnp.zeros_like(gram)
    coupled[...] = jnp.zeros_like(coupled)

    def use(piece, ref):
        value = ref[...]
        gram[...] += lax.dot_general(
            value, value, (((0,), (0,)), ((), ())), preferred_element_type=F32
        )
        coupled[...] += jnp.dot(blocks[piece], value, preferred_element_type=F32)

    spread(dims, cols, True, packed, buf, send_sem, recv_sem, use)


def tiles_kernel(dims, source, out, send_sem, recv_sem):
    def use(piece, ref):
        if ref is source:
            out[piece] = source[...]

    spread(dims, 1, False, source, out, send_sem, recv_sem, use)


def totals_kernel(dims, cols, source, out, buf, send_sem, recv_sem):
    out[...] = jnp.zeros_like(out)

    def use(piece, ref):
        out[...] += ref[...]

    spread(dims, cols, True, source, buf, send_sem, recv_sem, use)


def step_kernel(
    iteration, scale, gram, coupled, degree, current, lagrange, projected, stats,
    current_out, lagrange_out, projected_out, packed_out, stats_out, precond, inverse, rest,
):
    n = gram.shape[0]
    rows = lax.broadcasted_iota(jnp.int32, (n, n), 0)
    columns = lax.broadcasted_iota(jnp.int32, (n, n), 1)
    eye = jnp.where(rows == columns, 1.0, 0.0).astype(F32)
    matrix = scale * gram[...] + ridge_shift * eye
    precond[...] = matrix

    def exact(a, b):
        return jnp.dot(a, b, precision=HIGHEST, preferred_element_type=F32)

    def fast(a, b):
        return jnp.dot(
            a.astype(jnp.bfloat16), b.astype(jnp.bfloat16), preferred_element_type=F32
        )

    def size(value):
        return jnp.sum(value * value)

    guess = n / jnp.sum(matrix * eye)
    first = eye * guess
    remain = eye - guess * matrix
    value = first + guess * remain
    for turn in range(3):
        remain = eye - fast(precond[...], value)
        value = value + fast(value, remain)
    inverse[...] = value
    rest[...] = eye - exact(precond[...], value)
    error = size(rest[...])

    good = error < 0.25

    @pl.when(jnp.logical_not(good))
    def _():
        bound = jnp.max(jnp.sum(jnp.abs(precond[...]), axis=1, keepdims=True))
        inverse[...] = eye / bound
        rest[...] = eye - precond[...] / bound

    def unfinished(state):
        turn, left = state
        return jnp.logical_and(turn < 48, left > 1e-6)

    def turn_body(state):
        turn, left = state
        inverse[...] = inverse[...] + exact(inverse[...], rest[...])
        rest[...] = eye - exact(precond[...], inverse[...])
        return turn + 1, size(rest[...])

    lax.while_loop(unfinished, turn_body, (jnp.int32(0), jnp.where(good, error, 1e6)))

    now = current[...]
    widened = now.astype(jnp.bfloat16).astype(F32)
    gradient = degree[...] * widened - coupled[...]
    descent = 2.0 * gradient - lagrange[...] - penalty * (now - projected[...])
    solved = exact(descent, inverse[...])
    solved = solved + exact(solved, rest[...])
    now = now + step_size * solved
    current_out[...] = now
    packed_out[...] = now.astype(jnp.bfloat16)
    unit = unit_rows(now + lagrange[...] / penalty)
    projected_out[...] = unit
    mismatch = now - unit
    lagrange_out[...] = lagrange[...] + penalty * mismatch
    line = lax.broadcasted_iota(jnp.int32, stats.shape, 0)
    lane = lax.broadcasted_iota(jnp.int32, stats.shape, 1)
    here = line == iteration
    old = stats[...]
    old = jnp.where(here & (lane == 0), jnp.sum(widened * gradient), old)
    stats_out[...] = jnp.where(here & (lane == 1), jnp.sum(mismatch * mismatch), old)


def whole_specs(count):
    return [pl.BlockSpec(memory_space=VMEM)] * count


def local(tiles, slots, factor, dual):
    row_count = lax.axis_size("row")
    col_count = lax.axis_size("col")
    pieces = row_count * col_count
    piece_rows, columns = factor.shape
    vertices = piece_rows * pieces
    count = tiles.shape[2]
    ny = 2 ** (int(math.log2(col_count)) // 2)
    dims = (row_count // 2, col_count // ny, ny)
    flat = (row_count // 2, 1, 1)
    limit = 60 * 2**20

    def params(number):
        return pltpu.CompilerParams(
            collective_id=number, has_side_effects=True, vmem_limit_bytes=limit
        )

    def semaphores(number):
        return [pltpu.SemaphoreType.DMA((number,)), pltpu.SemaphoreType.DMA((number,))]

    weights = block_weights(tiles.reshape(count, piece_rows, piece_rows), vertices)
    stored = slots.reshape(1, -1).astype(jnp.bfloat16)
    stored = jnp.pad(stored, ((0, 15), (0, piece_rows - count)))
    payload = jnp.concatenate([weights.reshape(count * piece_rows, piece_rows), stored], axis=0)
    gathered = pl.pallas_call(
        functools.partial(tiles_kernel, flat),
        out_shape=jax.ShapeDtypeStruct((row_count,) + payload.shape, payload.dtype),
        in_specs=whole_specs(1),
        out_specs=pl.BlockSpec(memory_space=VMEM),
        scratch_shapes=semaphores(row_count),
        compiler_params=params(0),
    )(payload)
    mine = lax.axis_index("row")
    chosen = gathered[:, count * piece_rows, :count].astype(jnp.int32)
    wanted = jnp.arange(col_count, dtype=jnp.int32) * row_count + mine
    selector = (chosen[:, None, :] == wanted[None, :, None]).astype(jnp.bfloat16)
    source = gathered[:, : count * piece_rows].reshape(row_count, count, piece_rows, piece_rows)
    blocks = jnp.einsum("rat,rtij->raji", selector, source, preferred_element_type=jnp.bfloat16)
    blocks = blocks.reshape(pieces, piece_rows, piece_rows)
    degree = jnp.sum(blocks.astype(F32), axis=(0, 2)).reshape(piece_rows, 1)

    state = jax.ShapeDtypeStruct(factor.shape, F32)
    stats_shape = jax.ShapeDtypeStruct((8, 128), F32)
    gather = pl.pallas_call(
        functools.partial(gather_kernel, dims, col_count),
        out_shape=(jax.ShapeDtypeStruct((columns, columns), F32), state),
        in_specs=whole_specs(2),
        out_specs=tuple(whole_specs(2)),
        scratch_shapes=[VMEM((pieces, piece_rows, columns), jnp.bfloat16)] + semaphores(pieces),
        compiler_params=params(1),
    )
    current = factor
    lagrange = dual
    projected = unit_rows(current + lagrange / penalty)
    packed = factor.astype(jnp.bfloat16)
    stats = jnp.zeros((8, 128), F32)
    for iteration in range(ITERS):
        gram, coupled = gather(packed, blocks)
        current, lagrange, projected, packed, stats = pl.pallas_call(
            functools.partial(step_kernel, iteration, columns / vertices),
            out_shape=(
                state, state, state, jax.ShapeDtypeStruct(factor.shape, jnp.bfloat16), stats_shape,
            ),
            in_specs=whole_specs(7),
            out_specs=tuple(whole_specs(5)),
            scratch_shapes=[VMEM((columns, columns), F32)] * 3,
            compiler_params=pltpu.CompilerParams(vmem_limit_bytes=limit),
        )(gram, coupled, degree, current, lagrange, projected, stats)
    totals = pl.pallas_call(
        functools.partial(totals_kernel, dims, col_count),
        out_shape=stats_shape,
        in_specs=whole_specs(1),
        out_specs=pl.BlockSpec(memory_space=VMEM),
        scratch_shapes=[VMEM((pieces, 8, 128), F32)] + semaphores(pieces),
        compiler_params=params(2),
    )(stats)
    objective = totals[:ITERS, 0] / (4.0 * vertices)
    residual = totals[:ITERS, 1] / vertices
    return (current, lagrange, objective, residual)


def solution(mesh):
    in_specs = (
        P("row", "col", None, None, None),
        P("row", "col", None),
        P(("row", "col"), None),
        P(("row", "col"), None),
    )
    out_specs = (P(("row", "col"), None), P(("row", "col"), None), P(), P())
    return jax.shard_map(local, mesh=mesh, in_specs=in_specs, out_specs=out_specs, check_vma=False)
```

time: 673 us -> 165 us (0.25)
  waiting for transfers between devices: 354 us -> 0 us
  other arithmetic: 176 us -> 6.65 us
  Pallas kernels: 0 us -> 153 us
  blocking collectives: 80.4 us -> 0 us
  local copies, waits for them, and re-layouts: 25.8 us -> 3.25 us
  between operations: 21.1 us -> 0.73 us
  matrix products: 11.9 us -> 0.87 us
    psum x3 -> x0, waiting for transfers between devices: 352 us -> none  [local(): gram_total = lax.psum(own_gram, ('row', 'col'))]
    another operation x31 -> x0, other arithmetic: 166 us -> none  [the longest x20 103 us: local(): triangle = jnp.linalg.cholesky(precond)]
    pallas_call x0 -> x8, Pallas kernels: none -> 153 us  [the longest x3 73 us: local(): gram, coupled = gather(packed, blocks)]
    psum x1 -> x0, blocking collectives: 39.2 us -> none  [local(): stacked = lax.psum(stacked, ('row', 'col'))]
    unnamed x1 -> x0, blocking collectives: 22.3 us -> none
    all_gather x3 -> x0, blocking collectives: 18.8 us -> none  [local(): lax.all_gather(packed, 'row', axis=0, tiled=True)]
    another operation x28 -> x0, local copies, waits for them, and re-layouts: 12 us -> none  [the longest x22 12 us: local(): jax.scipy.linalg.cho_solve((triangle, True), descent.T)]
    unnamed x26 -> x2, local copies, waits for them, and re-layouts: 8.74 us -> 0.01 us
  transfers between devices with their start and end apart: 6 -> 0, of which waited for: 3 -> 0; matrix products, arithmetic and copies ran while one was open for 27% -> 0% of each run, Pallas kernels for 0% -> 0%
where the time goes in v1:
time: 165 us; the launch traced here: 164 us
  Pallas kernels  153 us (93%)
  other arithmetic  6.65 us (4%)
  local copies, waits for them, and re-layouts  3.25 us (2%)
    pallas_call x3, Pallas kernels, local(): gram, coupled = gather(packed, blocks)  73 us
    pallas_call x3, Pallas kernels, local(): pl.pallas_call(functools.partial(step_kernel, iteration, columns / vertic...  50 us
    pallas_call x1, Pallas kernels, local(): pl.pallas_call(functools.partial(totals_kernel, dims, col_count), out_sha...  16.4 us
    pallas_call x1, Pallas kernels, local(): pl.pallas_call(functools.partial(tiles_kernel, flat), out_shape=jax.Shape...  13.2 us

profile of v1, /device:TPU:0, one launch (start us, length us, event | category | flops | bytes accessed | tf_op | source)
XLA Modules:
  0.0 164.1 jit_solution(17782763459646741831)
XLA Ops:
  0.6 0.0 copy-start
  0.7 0.7 convert_bitcast_fusion
  1.4 1.1 multiply_reduce_fusion
  2.5 1.8 %broadcast_multiply_fusion = (f32[128,256]{1,0:T(8,128)}, bf16[128,256]{1,0:T(8,128)(2,1)}) fusion(f32[128]{0:T(128)S(1)} %add_rsqrt_fusion, f32[128,256]{1,0:T(8,128)} %current.1, f32[128,256]{1,0:T(8,128)} %lagrange.1), kind=kLoop, calls=%fused_computation.9 | loop fusion | flops 131072 | bytes 459264 | tf_op jit(solution)/shard_map/mul | solution.py:30
  4.2 0.0 copy-done
  4.2 0.1 multiply_convert_fusion
  4.3 0.7 fusion.2.source
  5.1 13.2 %shard_map.75 = bf16[4,1040,128]{2,1,0:T(8,128)(2,1)} custom-call(bf16[1040,128]{1,0:T(8,128)(2,1)} %fusion.2.source), custom_call_target="tpu_custom_call" | custom-call | tf_op jit(solution)/shard_map/pallas_call | solution.py:242
  18.3 0.0 slice-start
  18.3 0.8 slice_convert_fusion
  19.1 0.4 slice-done
  19.5 0.9 convert_reduce_fusion
  20.4 0.8 copy.15.degree
  21.1 1.5 copy.14
  22.6 24.2 %shard_map.76 = (f32[256,256]{1,0:T(8,128)}, f32[128,256]{1,0:T(8,128)}) custom-call(bf16[128,256]{1,0:T(8,128)(2,1)} %get-tuple-element.45.packed, bf16[32,128,128]{2,1,0:T(8,128)(2,1)} %bitcast.16), custom_call_target="tpu_custom_call" | custom-call | tf_op jit(solution)/shard_map/pallas_call | solution.py:275
  46.9 0.6 broadcast_in_dim.2.stats
  47.5 17.0 %shard_map.77 = (f32[128,256]{1,0:T(8,128)}, f32[128,256]{1,0:T(8,128)}, f32[128,256]{1,0:T(8,128)}, bf16[128,256]{1,0:T(8,128)(2,1)}, f32[8,128]{1,0:T(8,128)}) custom-call(f32[256,256]{1,0:T(8,128)} %get-tuple-element.23.gram, f32[128,256]{1,0:T(8,128)} %get-tuple-element.24.coupled, f32[128,1]{1,0:T(8,128)} %copy.15.degree, f32[128,256]{1,0:T(8,128)} %current.1, ...), custom_call_target="tpu_custom_call" | custom-call | tf_op jit(solution)/shard_map/pallas_call | solution.py:276
  64.5 24.1 %shard_map.78 = (f32[256,256]{1,0:T(8,128)}, f32[128,256]{1,0:T(8,128)}) custom-call(bf16[128,256]{1,0:T(8,128)(2,1)} %get-tuple-element.25.packed, bf16[32,128,128]{2,1,0:T(8,128)(2,1)} %bitcast.17), custom_call_target="tpu_custom_call" | custom-call | tf_op jit(solution)/shard_map/pallas_call | solution.py:275
  88.6 17.2 %shard_map.79 = (f32[128,256]{1,0:T(8,128)}, f32[128,256]{1,0:T(8,128)}, f32[128,256]{1,0:T(8,128)}, bf16[128,256]{1,0:T(8,128)(2,1)}, f32[8,128]{1,0:T(8,128)}) custom-call(f32[256,256]{1,0:T(8,128)} %get-tuple-element.26.gram, f32[128,256]{1,0:T(8,128)} %get-tuple-element.27.coupled, f32[128,1]{1,0:T(8,128)} %copy.15.degree, ...), custom_call_target="tpu_custom_call" | custom-call | tf_op jit(solution)/shard_map/pallas_call | solution.py:276
  105.8 24.6 %shard_map.80 = (f32[256,256]{1,0:T(8,128)}, f32[128,256]{1,0:T(8,128)}) custom-call(bf16[128,256]{1,0:T(8,128)(2,1)} %get-tuple-element.32.packed, bf16[32,128,128]{2,1,0:T(8,128)(2,1)} %bitcast.18), custom_call_target="tpu_custom_call" | custom-call | tf_op jit(solution)/shard_map/pallas_call | solution.py:275
  130.4 15.8 %shard_map.81 = (f32[128,256]{1,0:T(8,128)}, f32[128,256]{1,0:T(8,128)}, f32[128,256]{1,0:T(8,128)}, bf16[128,256]{1,0:T(8,128)(2,1)}, f32[8,128]{1,0:T(8,128)}) custom-call(f32[256,256]{1,0:T(8,128)} %get-tuple-element.33.gram, f32[128,256]{1,0:T(8,128)} %get-tuple-element.34.coupled, f32[128,1]{1,0:T(8,128)} %copy.15.degree, ...), custom_call_target="tpu_custom_call" | custom-call | tf_op jit(solution)/shard_map/pallas_call | solution.py:276
  146.2 16.4 %shard_map.82 = f32[8,128]{1,0:T(8,128)} custom-call(f32[8,128]{1,0:T(8,128)} %get-tuple-element.41.source), custom_call_target="tpu_custom_call" | custom-call | tf_op jit(solution)/shard_map/pallas_call | solution.py:286
  162.7 1.5 multiply_reduce_fusion.1
  (2 shorter events, 0.0 us)
Async XLA Ops:
  0.6 3.6 %copy-start = (s32[1,1,8,128,128]{4,3,2,1,0:T(8,128)S(1)}, s32[1,1,8,128,128]{4,3,2,1,0:T(8,128)}, u32[]{:S(2)}) copy-start(s32[1,1,8,128,128]{4,3,2,1,0:T(8,128)} %param.4) | copy-start | bytes 1572868
  18.3 1.2 slice-start

commit v2 on v1

--- a/solution.py
+++ b/solution.py
@@ -30,111 +30,212 @@
     return values * lax.rsqrt(jnp.sum(values * values, axis=1, keepdims=True) + 1e-06)
 
 
-def spread(dims, cols, whole, src, buf, send_sem, recv_sem, use):
+class Place:
+    def __init__(self, dims, cols, whole):
+        self.nx, self.nz, self.ny = dims
+        self.cols, self.whole = cols, whole
+        row, self.col = lax.axis_index("row"), lax.axis_index("col")
+        self.x, self.core = row // 2, row % 2
+        self.z, self.y = (self.col // self.ny, self.col % self.ny) if whole else (0, 0)
+        self.zs = [self.device(0, 0, d, 0) for d in range(1, self.nz)]
+        self.ys = [self.device(0, 0, 0, d) for d in range(1, self.ny)]
+        self.xs = [self.device(d, 0, 0, 0) for d in range(1, self.nx)]
+        self.twin = self.device(0, 1, 0, 0)
+        self.mates = self.zs + self.ys + self.xs + [self.twin]
+
+    def coordinates(self, dx, dk, dz, dy):
+        z, y = (self.z + dz) % self.nz, (self.y + dy) % self.ny
+        return ((self.x + dx) % self.nx) * 2 + (self.core + dk) % 2, z * self.ny + y
+
+    def device(self, dx, dk, dz, dy):
+        row, col = self.coordinates(dx, dk, dz, dy)
+        return {"row": row, "col": col if self.whole else self.col}
+
+    def piece(self, dx, dk, dz, dy):
+        row, col = self.coordinates(dx, dk, dz, dy)
+        return row * self.cols + col
+
+    def greet(self):
+        barrier = pltpu.get_barrier_semaphore()
+        for mate in self.mates:
+            pl.semaphore_signal(barrier, inc=1, device_id=mate, device_id_type=MESH)
+        pl.semaphore_wait(barrier, len(self.mates))
+
+
+def send(src, dst, send_sem, recv_sem, mate):
+    return pltpu.make_async_remote_copy(
+        src_ref=src,
+        dst_ref=dst,
+        send_sem=send_sem,
+        recv_sem=recv_sem,
+        device_id=mate,
+        device_id_type=MESH,
+    )
+
+
+def spread(dims, cols, whole, src, buf, send_sem, half_sem, recv_sem, use):
+    at = Place(dims, cols, whole)
     nx, nz, ny = dims
-    row, col = lax.axis_index("row"), lax.axis_index("col")
-    x, core = row // 2, row % 2
-    if whole:
-        z, y = col // ny, col % ny
-    else:
-        z = y = 0
-
-    def device(xx, kk, zz, yy):
-        return {"row": xx * 2 + kk, "col": zz * ny + yy if whole else col}
-
-    def piece_of(xx, kk, zz, yy):
-        return (xx * 2 + kk) * cols + zz * ny + yy
-
-    barrier = pltpu.get_barrier_semaphore()
-    mates = [device(x, core, (z + d) % nz, y) for d in range(1, nz)]
-    mates += [device(x, core, z, (y + d) % ny) for d in range(1, ny)]
-    mates += [device((x + d) % nx, core, z, y) for d in range(1, nx)]
-    mates += [device(x, 1 - core, z, y)]
-    for mate in mates:
-        pl.semaphore_signal(barrier, inc=1, device_id=mate, device_id_type=MESH)
-    pl.semaphore_wait(barrier, len(mates))
-
-    def copy(ref, piece, number, mate):
-        return pltpu.make_async_remote_copy(
-            src_ref=ref,
-            dst_ref=buf.at[piece],
-            send_sem=send_sem.at[number],
-            recv_sem=recv_sem.at[piece],
-            device_id=mate,
-            device_id_type=MESH,
-        )
-
-    me = piece_of(x, core, z, y)
-    for number, mate in enumerate(mates):
-        copy(src, me, number, mate).start()
-    use(me, src)
-
-    def place(m, kk):
-        return piece_of((x + m // (nz * ny)) % nx, kk, (z + m % nz) % nz, (y + m // nz % ny) % ny)
+    cut = src.shape[0] // 2
+    halves = (pl.ds(0, cut), pl.ds(cut, src.shape[0] - cut))
+    at.greet()
+
+    def start(ref, piece, number, mate):
+        send(ref, buf.at[piece], send_sem.at[number], recv_sem.at[0, piece], mate).start()
+
+    def start_half(side, piece, number, mate):
+        part = buf.at[piece, halves[side]]
+        send(part, part, half_sem.at[side, number], recv_sem.at[side, piece], mate).start()
 
     def arrive(piece):
-        copy(src, piece, 0, mates[-1]).wait_recv()
-
-    def stage(first, last, base, onward):
-        def body(m, carry):
-            piece = place(m, core)
+        send(src, buf.at[piece], send_sem.at[0], recv_sem.at[0, piece], at.twin).wait_recv()
+
+    def arrive_halves(piece):
+        for side in range(2):
+            part = buf.at[piece, halves[side]]
+            send(part, part, half_sem.at[side, 0], recv_sem.at[side, piece], at.twin).wait_recv()
+
+    along_z = lambda j: (0, j + 1, 0)
+    along_y = lambda j: (0, j % nz, 1 + j // nz)
+    along_x = lambda j: (1 + j // nz, j % nz, 0)
+    across = lambda j: (1 + j // (nz * (ny - 1)), j % nz, 1 + j // nz % (ny - 1))
+
+    base = 0
+    me = at.piece(0, 0, 0, 0)
+    for mate in at.mates:
+        start(src, me, base, mate)
+        base += 1
+
+    def piece_at(where, kk):
+        dx, dz, dy = where
+        return at.piece(dx, kk, dz, dy)
+
+    def handle_z(j, base):
+        piece = piece_at(along_z(j), 0)
+        arrive(piece)
+        onward = at.ys + at.xs + [at.twin]
+        for d, mate in enumerate(onward):
+            start(buf.at[piece], piece, base + j * len(onward) + d, mate)
+
+    def handle_side(place, side, onward):
+        def handle(j, base):
+            piece = piece_at(place(j), 0)
             arrive(piece)
             for d, mate in enumerate(onward):
-                copy(buf.at[piece], piece, base + (m - first) * len(onward) + d, mate).start()
-            use(piece, buf.at[piece])
-            other = place(m - 1, 1 - core)
-            arrive(other)
-            use(other, buf.at[other])
+                start_half(side, piece, j * len(onward) + d, mate)
+            start(buf.at[piece], piece, base + j, at.twin)
+
+        return handle
+
+    def handle_across(j, base):
+        piece = piece_at(across(j), 0)
+        arrive_halves(piece)
+        start(buf.at[piece], piece, base + j, at.twin)
+
+    count_y, count_x = nz * (ny - 1), nz * (nx - 1)
+    y_item = (along_y, handle_side(along_y, 0, at.xs), 1)
+    x_item = (along_x, handle_side(along_x, 1, at.ys), 1)
+    groups = [(nz - 1, [(along_z, handle_z, len(at.ys) + len(at.xs) + 1)])]
+    if count_y == count_x:
+        groups += [(count_y, [y_item, x_item])]
+    else:
+        groups += [(count_y, [y_item]), (count_x, [x_item])]
+    groups += [(nz * (ny - 1) * (nx - 1), [(across, handle_across, 1)])]
+
+    def both(where, ref=None):
+        twin = piece_at(where, 1)
+        arrive(twin)
+        piece = piece_at(where, 0)
+        use(piece, twin, buf.at[piece] if ref is None else ref)
+
+    late = [functools.partial(both, (0, 0, 0), src)]
+    for count, items in groups:
+        if count == 0:
+            continue
+        bases = []
+        for _, _, sends in items:
+            bases.append(base)
+            base += count * sends
+        for (_, handle, _), first in zip(items, bases):
+            handle(0, first)
+        for action in late:
+            action()
+
+        def body(j, carry, items=items, bases=bases):
+            for (_, handle, _), first in zip(items, bases):
+                handle(j, first)
+            for place, _, _ in items:
+                both(place(j - 1))
             return carry
 
-        if last > first:
-            lax.fori_loop(first, last, body, 0)
-        return base + (last - first) * len(onward)
-
-    base = len(mates)
-    base = stage(1, nz, base, mates[nz - 1 :])
-    base = stage(nz, nz * ny, base, mates[nz + ny - 2 :])
-    base = stage(nz * ny, nz * ny * nx, base, mates[-1:])
-    other = place(nz * ny * nx - 1, 1 - core)
-    arrive(other)
-    use(other, buf.at[other])
+        if count > 1:
+            lax.fori_loop(1, count, body, 0)
+        late = [functools.partial(both, place(count - 1)) for place, _, _ in items]
+    for action in late:
+        action()
 
     def drain(number, carry):
-        copy(src, me, number, mates[-1]).wait_send()
+        send(src, buf.at[me], send_sem.at[number], recv_sem.at[0, me], at.twin).wait_send()
         return carry
 
     lax.fori_loop(0, base, drain, 0)
-
-
-def gather_kernel(dims, cols, packed, blocks, gram, coupled, buf, send_sem, recv_sem):
+    for side, total in ((0, count_y * (nx - 1)), (1, count_x * (ny - 1))):
+
+        def drain_half(number, carry, side=side):
+            part = buf.at[me, halves[side]]
+            send(part, part, half_sem.at[side, number], recv_sem.at[side, me], at.twin).wait_send()
+            return carry
+
+        if total:
+            lax.fori_loop(0, total, drain_half, 0)
+
+
+def gather_kernel(dims, cols, packed, blocks, gram, coupled, buf, send_sem, half_sem, recv_sem):
     gram[...] = jnp.zeros_like(gram)
     coupled[...] = jnp.zeros_like(coupled)
 
-    def use(piece, ref):
-        value = ref[...]
+    def use(piece, twin, ref):
+        value = jnp.concatenate([ref[...], buf[twin]], axis=0)
+        weights = jnp.concatenate([blocks[piece], blocks[twin]], axis=1)
         gram[...] += lax.dot_general(
             value, value, (((0,), (0,)), ((), ())), preferred_element_type=F32
         )
-        coupled[...] += jnp.dot(blocks[piece], value, preferred_element_type=F32)
-
-    spread(dims, cols, True, packed, buf, send_sem, recv_sem, use)
-
-
-def tiles_kernel(dims, source, out, send_sem, recv_sem):
-    def use(piece, ref):
+        coupled[...] += jnp.dot(weights, value, preferred_element_type=F32)
+
+    spread(dims, cols, True, packed, buf, send_sem, half_sem, recv_sem, use)
+
+
+def tiles_kernel(dims, source, out, send_sem, half_sem, recv_sem):
+    def use(piece, twin, ref):
         if ref is source:
             out[piece] = source[...]
 
-    spread(dims, 1, False, source, out, send_sem, recv_sem, use)
-
-
-def totals_kernel(dims, cols, source, out, buf, send_sem, recv_sem):
-    out[...] = jnp.zeros_like(out)
-
-    def use(piece, ref):
-        out[...] += ref[...]
-
-    spread(dims, cols, True, source, buf, send_sem, recv_sem, use)
+    spread(dims, 1, False, source, out, send_sem, half_sem, recv_sem, use)
+
+
+def totals_kernel(dims, cols, source, out, sums, buf, send_sem, recv_sem):
+    at = Place(dims, cols, True)
+    at.greet()
+    total = source[...]
+    first = 0
+    copies = []
+    for stage, mates in enumerate((at.zs, at.ys, at.xs, [at.twin])):
+        held = source if stage == 0 else sums.at[stage]
+        if stage:
+            sums[stage] = total
+        here = []
+        for d, mate in enumerate(mates):
+            slot = first + d
+            here.append(send(held, buf.at[slot], send_sem.at[slot], recv_sem.at[slot], mate))
+            here[-1].start()
+        for d, copy in enumerate(here):
+            copy.wait_recv()
+            total = total + buf[first + d]
+        copies += here
+        first += len(mates)
+    out[...] = total
+    for copy in copies:
+        copy.wait_send()
 
 
 def step_kernel(
@@ -193,7 +294,11 @@
     now = current[...]
     widened = now.astype(jnp.bfloat16).astype(F32)
     gradient = degree[...] * widened - coupled[...]
-    descent = 2.0 * gradient - lagrange[...] - penalty * (now - projected[...])
+    if iteration == 0:
+        before = unit_rows(now + lagrange[...] / penalty)
+    else:
+        before = projected[...]
+    descent = 2.0 * gradient - lagrange[...] - penalty * (now - before)
     solved = exact(descent, inverse[...])
     solved = solved + exact(solved, rest[...])
     now = now + step_size * solved
@@ -206,7 +311,7 @@
     line = lax.broadcasted_iota(jnp.int32, stats.shape, 0)
     lane = lax.broadcasted_iota(jnp.int32, stats.shape, 1)
     here = line == iteration
-    old = stats[...]
+    old = jnp.zeros(stats.shape, F32) if iteration == 0 else stats[...]
     old = jnp.where(here & (lane == 0), jnp.sum(widened * gradient), old)
     stats_out[...] = jnp.where(here & (lane == 1), jnp.sum(mismatch * mismatch), old)
 
@@ -233,7 +338,8 @@
         )
 
     def semaphores(number):
-        return [pltpu.SemaphoreType.DMA((number,)), pltpu.SemaphoreType.DMA((number,))]
+        dma = pltpu.SemaphoreType.DMA
+        return [dma((number,)), dma((2, number)), dma((2, number))]
 
     weights = block_weights(tiles.reshape(count, piece_rows, piece_rows), vertices)
     stored = slots.reshape(1, -1).astype(jnp.bfloat16)
@@ -268,9 +374,9 @@
     )
     current = factor
     lagrange = dual
-    projected = unit_rows(current + lagrange / penalty)
+    projected = dual
     packed = factor.astype(jnp.bfloat16)
-    stats = jnp.zeros((8, 128), F32)
+    stats = dual[:8, :128]
     for iteration in range(ITERS):
         gram, coupled = gather(packed, blocks)
         current, lagrange, projected, packed, stats = pl.pallas_call(
@@ -288,7 +394,8 @@
         out_shape=stats_shape,
         in_specs=whole_specs(1),
         out_specs=pl.BlockSpec(memory_space=VMEM),
-        scratch_shapes=[VMEM((pieces, 8, 128), F32)] + semaphores(pieces),
+        scratch_shapes=[VMEM((4, 8, 128), F32), VMEM((pieces, 8, 128), F32)]
+        + [pltpu.SemaphoreType.DMA((pieces,))] * 2,
         compiler_params=params(2),
     )(stats)
     objective = totals[:ITERS, 0] / (4.0 * vertices)

time: 165 us -> 160 us (0.970); the launches traced: 164 us -> 161 us
  Pallas kernels: 153 us -> 149 us
    pallas_call x3, Pallas kernels: 73 us -> 70.2 us  [local(): gram, coupled = gather(packed, blocks)]
    pallas_call x1, Pallas kernels: 16.4 us -> 14.6 us  [local(): pl.pallas_call(functools.partial(totals_kernel, dims, col_count), out_sha...]
    mul x1 -> x0, other arithmetic: 1.78 us -> none  [unit_rows(): values * lax.rsqrt(jnp.sum(values * values, axis=1, keepdims=True) + 1e-06)]
where the time goes in v2:
time: 160 us; the launch traced here: 161 us
  Pallas kernels  149 us (93%)
  other arithmetic  6.31 us (4%)
  local copies, waits for them, and re-layouts  3.91 us (2%)
    pallas_call x3, Pallas kernels, local(): gram, coupled = gather(packed, blocks)  70.2 us
    pallas_call x3, Pallas kernels, local(): pl.pallas_call(functools.partial(step_kernel, iteration, columns / vertic...  51.2 us
    pallas_call x1, Pallas kernels, local(): pl.pallas_call(functools.partial(totals_kernel, dims, col_count), out_sha...  14.6 us
    pallas_call x1, Pallas kernels, local(): pl.pallas_call(functools.partial(tiles_kernel, flat), out_shape=jax.Shape...  13.3 us

profile of v2, /device:TPU:0, one launch (start us, length us, event | category | flops | bytes accessed | tf_op | source)
XLA Modules:
  0.0 161.1 jit_solution(7093292747585911412)
XLA Ops:
  0.6 0.7 convert_bitcast_fusion
  1.3 1.3 slice.17.stats
  2.6 1.5 convert_element_type.38.packed
  4.1 1.1 multiply_convert_fusion
  5.2 0.7 fusion.2.source
  6.0 13.3 %shard_map.75 = bf16[4,1040,128]{2,1,0:T(8,128)(2,1)} custom-call(bf16[1040,128]{1,0:T(8,128)(2,1)} %fusion.2.source), custom_call_target="tpu_custom_call" | custom-call | tf_op jit(solution)/shard_map/pallas_call | solution.py:348
  19.3 0.0 slice-start
  19.3 0.8 slice_convert_fusion
  20.1 0.4 slice-done
  20.5 0.9 convert_reduce_fusion
  21.4 0.7 copy.15.degree
  22.1 1.4 copy.14
  23.6 23.7 %shard_map.76 = (f32[256,256]{1,0:T(8,128)}, f32[128,256]{1,0:T(8,128)}) custom-call(bf16[128,256]{1,0:T(8,128)(2,1)} %convert_element_type.38.packed, bf16[32,128,128]{2,1,0:T(8,128)(2,1)} %bitcast.16), custom_call_target="tpu_custom_call" | custom-call | tf_op jit(solution)/shard_map/pallas_call | solution.py:381
  47.3 17.1 %shard_map.77 = (f32[128,256]{1,0:T(8,128)}, f32[128,256]{1,0:T(8,128)}, f32[128,256]{1,0:T(8,128)}, bf16[128,256]{1,0:T(8,128)(2,1)}, f32[8,128]{1,0:T(8,128)}) custom-call(f32[256,256]{1,0:T(8,128)} %get-tuple-element.23.gram, f32[128,256]{1,0:T(8,128)} %get-tuple-element.24.coupled, f32[128,1]{1,0:T(8,128)} %copy.15.degree, f32[128,256]{1,0:T(8,128)} %current.1, ...), custom_call_target="tpu_custom_call" | custom-call | tf_op jit(solution)/shard_map/pallas_call | solution.py:382
  64.4 23.1 %shard_map.78 = (f32[256,256]{1,0:T(8,128)}, f32[128,256]{1,0:T(8,128)}) custom-call(bf16[128,256]{1,0:T(8,128)(2,1)} %get-tuple-element.25.packed, bf16[32,128,128]{2,1,0:T(8,128)(2,1)} %bitcast.17), custom_call_target="tpu_custom_call" | custom-call | tf_op jit(solution)/shard_map/pallas_call | solution.py:381
  87.5 17.2 %shard_map.79 = (f32[128,256]{1,0:T(8,128)}, f32[128,256]{1,0:T(8,128)}, f32[128,256]{1,0:T(8,128)}, bf16[128,256]{1,0:T(8,128)(2,1)}, f32[8,128]{1,0:T(8,128)}) custom-call(f32[256,256]{1,0:T(8,128)} %get-tuple-element.26.gram, f32[128,256]{1,0:T(8,128)} %get-tuple-element.27.coupled, f32[128,1]{1,0:T(8,128)} %copy.15.degree, ...), custom_call_target="tpu_custom_call" | custom-call | tf_op jit(solution)/shard_map/pallas_call | solution.py:382
  104.7 23.3 %shard_map.80 = (f32[256,256]{1,0:T(8,128)}, f32[128,256]{1,0:T(8,128)}) custom-call(bf16[128,256]{1,0:T(8,128)(2,1)} %get-tuple-element.32.packed, bf16[32,128,128]{2,1,0:T(8,128)(2,1)} %bitcast.18), custom_call_target="tpu_custom_call" | custom-call | tf_op jit(solution)/shard_map/pallas_call | solution.py:381
  128.0 17.0 %shard_map.81 = (f32[128,256]{1,0:T(8,128)}, f32[128,256]{1,0:T(8,128)}, f32[128,256]{1,0:T(8,128)}, bf16[128,256]{1,0:T(8,128)(2,1)}, f32[8,128]{1,0:T(8,128)}) custom-call(f32[256,256]{1,0:T(8,128)} %get-tuple-element.33.gram, f32[128,256]{1,0:T(8,128)} %get-tuple-element.34.coupled, f32[128,1]{1,0:T(8,128)} %copy.15.degree, ...), custom_call_target="tpu_custom_call" | custom-call | tf_op jit(solution)/shard_map/pallas_call | solution.py:382
  145.0 14.6 %shard_map.82 = f32[8,128]{1,0:T(8,128)} custom-call(f32[8,128]{1,0:T(8,128)} %get-tuple-element.41.source), custom_call_target="tpu_custom_call" | custom-call | tf_op jit(solution)/shard_map/pallas_call | solution.py:392
  159.6 1.5 multiply_reduce_fusion
  (1 shorter events, 0.0 us)
Async XLA Ops:
  19.3 1.2 slice-start

commit v3 on v2

--- a/solution.py
+++ b/solution.py
@@ -55,11 +55,11 @@
         row, col = self.coordinates(dx, dk, dz, dy)
         return row * self.cols + col
 
-    def greet(self):
+    def greet(self, mates):
         barrier = pltpu.get_barrier_semaphore()
-        for mate in self.mates:
+        for mate in mates:
             pl.semaphore_signal(barrier, inc=1, device_id=mate, device_id_type=MESH)
-        pl.semaphore_wait(barrier, len(self.mates))
+        pl.semaphore_wait(barrier, len(mates))
 
 
 def send(src, dst, send_sem, recv_sem, mate):
@@ -73,12 +73,12 @@
     )
 
 
-def spread(dims, cols, whole, src, buf, send_sem, half_sem, recv_sem, use):
+def spread(dims, cols, whole, src, buf, send_sem, half_sem, recv_sem, use, prelude=None):
     at = Place(dims, cols, whole)
     nx, nz, ny = dims
     cut = src.shape[0] // 2
     halves = (pl.ds(0, cut), pl.ds(cut, src.shape[0] - cut))
-    at.greet()
+    at.greet(at.mates)
 
     def start(ref, piece, number, mate):
         send(ref, buf.at[piece], send_sem.at[number], recv_sem.at[0, piece], mate).start()
@@ -105,6 +105,8 @@
     for mate in at.mates:
         start(src, me, base, mate)
         base += 1
+    if prelude is not None:
+        prelude(at)
 
     def piece_at(where, kk):
         dx, dz, dy = where
@@ -205,36 +207,73 @@
     spread(dims, cols, True, packed, buf, send_sem, half_sem, recv_sem, use)
 
 
-def tiles_kernel(dims, source, out, send_sem, half_sem, recv_sem):
+def first_kernel(
+    dims, cols, vertices, tiles, places, factor, gram, gathered, shelves,
+    packed, payload, send_sem, half_sem, recv_sem, tile_send, tile_recv,
+):
+    rows = payload.shape[0] - places.shape[0]
+    packed[...] = factor[...].astype(jnp.bfloat16)
+    payload[:rows] = block_weights(tiles[...], vertices)
+    payload[rows:] = places[...]
+    gram[...] = jnp.zeros_like(gram)
+    nx = dims[0]
+    chips = []
+
+    def shelf(at, dx, dk):
+        return at.coordinates(dx, dk, 0, 0)[0]
+
+    def tile_copy(at, ref, row, number, mate):
+        return send(ref, shelves.at[row], tile_send.at[number], tile_recv.at[row], mate)
+
+    def prelude(at):
+        chips.append(at)
+        row = shelf(at, 0, 0)
+        for number, mate in enumerate(at.xs + [at.twin]):
+            tile_copy(at, payload, row, number, mate).start()
+        shelves[row] = payload[...]
+        gathered[at.piece(0, 0, 0, 0)] = packed[...]
+
     def use(piece, twin, ref):
-        if ref is source:
-            out[piece] = source[...]
-
-    spread(dims, 1, False, source, out, send_sem, half_sem, recv_sem, use)
-
-
-def totals_kernel(dims, cols, source, out, sums, buf, send_sem, recv_sem):
+        value = jnp.concatenate([ref[...], gathered[twin]], axis=0)
+        gram[...] += lax.dot_general(
+            value, value, (((0,), (0,)), ((), ())), preferred_element_type=F32
+        )
+
+    spread(dims, cols, True, packed, gathered, send_sem, half_sem, recv_sem, use, prelude)
+    at = chips[0]
+    for d in range(1, nx):
+        row = shelf(at, d, 0)
+        tile_copy(at, payload, row, 0, at.twin).wait_recv()
+        tile_copy(at, shelves.at[row], row, nx - 1 + d, at.twin).start()
+    for d in range(nx):
+        tile_copy(at, payload, shelf(at, d, 1), 0, at.twin).wait_recv()
+    for number in range(2 * nx - 1):
+        tile_copy(at, payload, shelf(at, 0, 0), number, at.twin).wait_send()
+
+
+def totals_kernel(dims, cols, source, out, held, buf, send_sem, recv_sem):
     at = Place(dims, cols, True)
-    at.greet()
-    total = source[...]
-    first = 0
-    copies = []
-    for stage, mates in enumerate((at.zs, at.ys, at.xs, [at.twin])):
-        held = source if stage == 0 else sums.at[stage]
-        if stage:
-            sums[stage] = total
-        here = []
-        for d, mate in enumerate(mates):
-            slot = first + d
-            here.append(send(held, buf.at[slot], send_sem.at[slot], recv_sem.at[slot], mate))
-            here[-1].start()
-        for d, copy in enumerate(here):
+    nx, nz, ny = dims
+    far = [at.device(0, 0, i // ny, i % ny) for i in range(1, nz * ny)]
+    near = [at.device(i // 2, i % 2, 0, 0) for i in range(1, 2 * nx)]
+    at.greet(far + near)
+
+    def exchange(ref, mates, first):
+        copies = [
+            send(ref, buf.at[first + d], send_sem.at[first + d], recv_sem.at[first + d], mate)
+            for d, mate in enumerate(mates)
+        ]
+        for copy in copies:
+            copy.start()
+        total = ref[...]
+        for d, copy in enumerate(copies):
             copy.wait_recv()
             total = total + buf[first + d]
-        copies += here
-        first += len(mates)
-    out[...] = total
-    for copy in copies:
+        return copies, total
+
+    sent, held[...] = exchange(source, far, 0)
+    more, out[...] = exchange(held, near, len(far))
+    for copy in sent + more:
         copy.wait_send()
 
 
@@ -308,10 +347,10 @@
     projected_out[...] = unit
     mismatch = now - unit
     lagrange_out[...] = lagrange[...] + penalty * mismatch
-    line = lax.broadcasted_iota(jnp.int32, stats.shape, 0)
-    lane = lax.broadcasted_iota(jnp.int32, stats.shape, 1)
+    line = lax.broadcasted_iota(jnp.int32, stats_out.shape, 0)
+    lane = lax.broadcasted_iota(jnp.int32, stats_out.shape, 1)
     here = line == iteration
-    old = jnp.zeros(stats.shape, F32) if iteration == 0 else stats[...]
+    old = jnp.zeros(stats_out.shape, F32) if iteration == 0 else stats[...]
     old = jnp.where(here & (lane == 0), jnp.sum(widened * gradient), old)
     stats_out[...] = jnp.where(here & (lane == 1), jnp.sum(mismatch * mismatch), old)
 
@@ -329,7 +368,6 @@
     count = tiles.shape[2]
     ny = 2 ** (int(math.log2(col_count)) // 2)
     dims = (row_count // 2, col_count // ny, ny)
-    flat = (row_count // 2, 1, 1)
     limit = 60 * 2**20
 
     def params(number):
@@ -341,18 +379,26 @@
         dma = pltpu.SemaphoreType.DMA
         return [dma((number,)), dma((2, number)), dma((2, number))]
 
-    weights = block_weights(tiles.reshape(count, piece_rows, piece_rows), vertices)
-    stored = slots.reshape(1, -1).astype(jnp.bfloat16)
-    stored = jnp.pad(stored, ((0, 15), (0, piece_rows - count)))
-    payload = jnp.concatenate([weights.reshape(count * piece_rows, piece_rows), stored], axis=0)
-    gathered = pl.pallas_call(
-        functools.partial(tiles_kernel, flat),
-        out_shape=jax.ShapeDtypeStruct((row_count,) + payload.shape, payload.dtype),
-        in_specs=whole_specs(1),
-        out_specs=pl.BlockSpec(memory_space=VMEM),
-        scratch_shapes=semaphores(row_count),
+    places = jnp.pad(
+        slots.reshape(1, -1).astype(jnp.bfloat16), ((0, 15), (0, piece_rows - count))
+    )
+    gram, everything, gathered = pl.pallas_call(
+        functools.partial(first_kernel, dims, col_count, vertices),
+        out_shape=(
+            jax.ShapeDtypeStruct((columns, columns), F32),
+            jax.ShapeDtypeStruct((pieces, piece_rows, columns), jnp.bfloat16),
+            jax.ShapeDtypeStruct((row_count, count * piece_rows + 16, piece_rows), jnp.bfloat16),
+        ),
+        in_specs=whole_specs(3),
+        out_specs=tuple(whole_specs(3)),
+        scratch_shapes=[
+            VMEM((piece_rows, columns), jnp.bfloat16),
+            VMEM((count * piece_rows + 16, piece_rows), jnp.bfloat16),
+        ]
+        + semaphores(pieces)
+        + [pltpu.SemaphoreType.DMA((row_count,))] * 2,
         compiler_params=params(0),
-    )(payload)
+    )(tiles.reshape(count * piece_rows, piece_rows), places, factor)
     mine = lax.axis_index("row")
     chosen = gathered[:, count * piece_rows, :count].astype(jnp.int32)
     wanted = jnp.arange(col_count, dtype=jnp.int32) * row_count + mine
@@ -375,10 +421,11 @@
     current = factor
     lagrange = dual
     projected = dual
-    packed = factor.astype(jnp.bfloat16)
-    stats = dual[:8, :128]
+    stats = degree
+    coupled = jnp.einsum("pij,pjk->ik", blocks, everything, preferred_element_type=F32)
     for iteration in range(ITERS):
-        gram, coupled = gather(packed, blocks)
+        if iteration:
+            gram, coupled = gather(packed, blocks)
         current, lagrange, projected, packed, stats = pl.pallas_call(
             functools.partial(step_kernel, iteration, columns / vertices),
             out_shape=(
@@ -394,7 +441,7 @@
         out_shape=stats_shape,
         in_specs=whole_specs(1),
         out_specs=pl.BlockSpec(memory_space=VMEM),
-        scratch_shapes=[VMEM((4, 8, 128), F32), VMEM((pieces, 8, 128), F32)]
+        scratch_shapes=[VMEM((8, 128), F32), VMEM((pieces, 8, 128), F32)]
         + [pltpu.SemaphoreType.DMA((pieces,))] * 2,
         compiler_params=params(2),
     )(stats)

time: 160 us -> 147 us (0.919)
  Pallas kernels: 149 us -> 136 us
  other arithmetic: 6.31 us -> 2.84 us
  matrix products: 0.87 us -> 2.84 us
    pallas_call x3 -> x2, Pallas kernels: 70.2 us -> 43.6 us  [local(): gram, coupled = gather(packed, blocks)]
    pallas_call x1, Pallas kernels: 13.3 us -> 29.9 us  [local(): pl.pallas_call(functools.partial(first_kernel, dims, col_count, vertices)...]
    convert_element_type x3 -> x1, other arithmetic: 3.31 us -> 0.66 us  [local(): slots.reshape(1, -1).astype(jnp.bfloat16)]
    pallas_call x1, Pallas kernels: 14.6 us -> 12.2 us  [local(): pl.pallas_call(functools.partial(totals_kernel, dims, col_count), out_sha...]
where the time goes in v3:
time: 147 us
  Pallas kernels  136 us (93%)
  local copies, waits for them, and re-layouts  4.4 us (3%)
  other arithmetic  2.84 us (2%)
  matrix products  2.84 us (2%)
    pallas_call x3, Pallas kernels, local(): pl.pallas_call(functools.partial(step_kernel, iteration, columns / vertic...  50.1 us
    pallas_call x2, Pallas kernels, local(): gram, coupled = gather(packed, blocks)  43.6 us
    pallas_call x1, Pallas kernels, local(): pl.pallas_call(functools.partial(first_kernel, dims, col_count, vertices)...  29.9 us
    pallas_call x1, Pallas kernels, local(): pl.pallas_call(functools.partial(totals_kernel, dims, col_count), out_sha...  12.2 us

profile of v3, /device:TPU:0, one launch (start us, length us, event | category | flops | bytes accessed | tf_op | source)
XLA Modules:
  0.0 146.6 jit_solution(4982334817681065854)
XLA Ops:
  0.6 0.7 convert_bitcast_fusion
  1.3 0.6 pad.4.places
  1.9 29.9 %shard_map.75 = (f32[256,256]{1,0:T(8,128)}, bf16[32,128,256]{2,1,0:T(8,128)(2,1)}, bf16[4,1040,128]{2,1,0:T(8,128)(2,1)}) custom-call(s32[1024,128]{1,0:T(8,128)} %bitcast.24, bf16[16,128]{1,0:T(8,128)(2,1)} %pad.4.places, f32[128,256]{1,0:T(8,128)} %current.1), custom_call_target="tpu_custom_call" | custom-call | tf_op jit(solution)/shard_map/pallas_call | solution.py:385
  31.8 1.3 slice.12
  33.1 0.7 slice_convert_fusion
  33.8 0.0 copy-start.1
  33.8 1.7 %convert_reduce_fusion = (f32[128]{0:T(128)S(1)}, bf16[4,8,128,128]{2,1,3,0:T(8,128)(2,1)}) fusion(s32[4,8]{1,0:T(4,128)S(1)} %bitcast.25, s32[8]{0:T(128)S(1)} %multiply_add_fusion, bf16[4,8,128,128]{3,2,1,0:T(8,128)(2,1)S(1)} %bitcast.23), kind=kOutput, calls=%fused_computation | convolution fusion | flops 9437312 | bytes 2097824 | tf_op jit(solution)/shard_map/rat,rtij->raji/dot_general | solution.py:407
  35.6 1.8 %copy.15 = bf16[4,8,128,128]{3,2,1,0:T(8,128)(2,1)S(1)} copy(bf16[4,8,128,128]{2,1,3,0:T(8,128)(2,1)} %get-tuple-element.47) | data formatting | bytes 2097152 | tf_op jit(solution)/shard_map/rat,rtij->raji/transpose | solution.py:407
  37.3 0.0 copy-start
  37.3 0.0 copy-done.1
  37.3 1.1 convolution_bitcast_fusion.1.coupled
  38.4 0.7 copy.16.degree.stats
  39.2 17.1 %shard_map.76 = (f32[128,256]{1,0:T(8,128)}, f32[128,256]{1,0:T(8,128)}, f32[128,256]{1,0:T(8,128)}, bf16[128,256]{1,0:T(8,128)(2,1)}, f32[8,128]{1,0:T(8,128)}) custom-call(f32[256,256]{1,0:T(8,128)} %get-tuple-element.24.gram, f32[128,256]{1,0:T(8,128)} %convolution_bitcast_fusion.1.coupled, f32[128,1]{1,0:T(8,128)} %copy.16.degree.stats, ...), custom_call_target="tpu_custom_call" | custom-call | tf_op jit(solution)/shard_map/pallas_call | solution.py:429
  56.2 0.0 copy-done
  56.2 20.4 %shard_map.77 = (f32[256,256]{1,0:T(8,128)}, f32[128,256]{1,0:T(8,128)}) custom-call(bf16[128,256]{1,0:T(8,128)(2,1)} %get-tuple-element.27.packed, bf16[32,128,128]{2,1,0:T(8,128)(2,1)} %bitcast.21), custom_call_target="tpu_custom_call" | custom-call | tf_op jit(solution)/shard_map/pallas_call | solution.py:428
  76.6 17.2 %shard_map.78 = (f32[128,256]{1,0:T(8,128)}, f32[128,256]{1,0:T(8,128)}, f32[128,256]{1,0:T(8,128)}, bf16[128,256]{1,0:T(8,128)(2,1)}, f32[8,128]{1,0:T(8,128)}) custom-call(f32[256,256]{1,0:T(8,128)} %get-tuple-element.28.gram, f32[128,256]{1,0:T(8,128)} %get-tuple-element.29.coupled, f32[128,1]{1,0:T(8,128)} %copy.16.degree.stats, ...), custom_call_target="tpu_custom_call" | custom-call | tf_op jit(solution)/shard_map/pallas_call | solution.py:429
  93.8 23.2 %shard_map.79 = (f32[256,256]{1,0:T(8,128)}, f32[128,256]{1,0:T(8,128)}) custom-call(bf16[128,256]{1,0:T(8,128)(2,1)} %get-tuple-element.34.packed, bf16[32,128,128]{2,1,0:T(8,128)(2,1)} %bitcast.22), custom_call_target="tpu_custom_call" | custom-call | tf_op jit(solution)/shard_map/pallas_call | solution.py:428
  117.0 15.8 %shard_map.80 = (f32[128,256]{1,0:T(8,128)}, f32[128,256]{1,0:T(8,128)}, f32[128,256]{1,0:T(8,128)}, bf16[128,256]{1,0:T(8,128)(2,1)}, f32[8,128]{1,0:T(8,128)}) custom-call(f32[256,256]{1,0:T(8,128)} %get-tuple-element.35.gram, f32[128,256]{1,0:T(8,128)} %get-tuple-element.36.coupled, f32[128,1]{1,0:T(8,128)} %copy.16.degree.stats, ...), custom_call_target="tpu_custom_call" | custom-call | tf_op jit(solution)/shard_map/pallas_call | solution.py:429
  132.9 12.2 %shard_map.81 = f32[8,128]{1,0:T(8,128)} custom-call(f32[8,128]{1,0:T(8,128)} %get-tuple-element.43.source), custom_call_target="tpu_custom_call" | custom-call | tf_op jit(solution)/shard_map/pallas_call | solution.py:439
  145.1 1.5 %multiply_reduce_fusion = (f32[3]{0:T(128)}, f32[3]{0:T(128)}) fusion(f32[8,128]{1,0:T(8,128)} %shard_map.81), kind=kLoop, calls=%fused_computation.8 | loop fusion | flops 6 | bytes 48 | tf_op jit(solution)/shard_map/div | solution.py:449
  (1 shorter events, 0.0 us)
Async XLA Ops:
  33.8 3.5 %copy-start.1 = (bf16[32,128,256]{2,1,0:T(8,128)(2,1)S(1)}, bf16[32,128,256]{2,1,0:T(8,128)(2,1)}, u32[]{:S(2)}) copy-start(bf16[32,128,256]{2,1,0:T(8,128)(2,1)} %get-tuple-element.26) | copy-start | bytes 6291460
  37.3 18.9 %copy-start = (bf16[4,8,128,128]{3,2,1,0:T(8,128)(2,1)}, bf16[4,8,128,128]{3,2,1,0:T(8,128)(2,1)S(1)}, u32[]{:S(2)}) copy-start(bf16[4,8,128,128]{3,2,1,0:T(8,128)(2,1)S(1)} %copy.15) | copy-start | bytes 3145732

commit v4 on v3

--- a/solution.py
+++ b/solution.py
@@ -198,11 +198,13 @@
 
     def use(piece, twin, ref):
         value = jnp.concatenate([ref[...], buf[twin]], axis=0)
-        weights = jnp.concatenate([blocks[piece], blocks[twin]], axis=1)
+        weights = jnp.concatenate([blocks[piece], blocks[twin]], axis=0)
         gram[...] += lax.dot_general(
             value, value, (((0,), (0,)), ((), ())), preferred_element_type=F32
         )
-        coupled[...] += jnp.dot(weights, value, preferred_element_type=F32)
+        coupled[...] += lax.dot_general(
+            weights, value, (((0,), (0,)), ((), ())), preferred_element_type=F32
+        )
 
     spread(dims, cols, True, packed, buf, send_sem, half_sem, recv_sem, use)
 
@@ -404,9 +406,9 @@
     wanted = jnp.arange(col_count, dtype=jnp.int32) * row_count + mine
     selector = (chosen[:, None, :] == wanted[None, :, None]).astype(jnp.bfloat16)
     source = gathered[:, : count * piece_rows].reshape(row_count, count, piece_rows, piece_rows)
-    blocks = jnp.einsum("rat,rtij->raji", selector, source, preferred_element_type=jnp.bfloat16)
+    blocks = jnp.einsum("rat,rtij->raij", selector, source, preferred_element_type=jnp.bfloat16)
     blocks = blocks.reshape(pieces, piece_rows, piece_rows)
-    degree = jnp.sum(blocks.astype(F32), axis=(0, 2)).reshape(piece_rows, 1)
+    degree = jnp.sum(blocks.astype(F32), axis=(0, 1)).reshape(piece_rows, 1)
 
     state = jax.ShapeDtypeStruct(factor.shape, F32)
     stats_shape = jax.ShapeDtypeStruct((8, 128), F32)
@@ -422,7 +424,7 @@
     lagrange = dual
     projected = dual
     stats = degree
-    coupled = jnp.einsum("pij,pjk->ik", blocks, everything, preferred_element_type=F32)
+    coupled = jnp.einsum("pji,pjk->ik", blocks, everything, preferred_element_type=F32)
     for iteration in range(ITERS):
         if iteration:
             gram, coupled = gather(packed, blocks)

time: 147 us -> 146 us (level)
    transpose x1 -> x0, local copies, waits for them, and re-layouts: 1.75 us -> none  [local(): jnp.einsum('rat,rtij->raji', selector, source, preferred_element_type=jnp...]
where the time goes in v4:
time: 146 us
  Pallas kernels  137 us (94%)
  local copies, waits for them, and re-layouts  3.35 us (2%)
  other arithmetic  2.84 us (2%)
  matrix products  2.04 us (1%)
    pallas_call x3, Pallas kernels, local(): pl.pallas_call(functools.partial(step_kernel, iteration, columns / vertic...  51.3 us
    pallas_call x2, Pallas kernels, local(): gram, coupled = gather(packed, blocks)  43.6 us
    pallas_call x1, Pallas kernels, local(): pl.pallas_call(functools.partial(first_kernel, dims, col_count, vertices)...  29.9 us
    pallas_call x1, Pallas kernels, local(): pl.pallas_call(functools.partial(totals_kernel, dims, col_count), out_sha...  12.3 us

profile of v4, /device:TPU:0, one launch (start us, length us, event | category | flops | bytes accessed | tf_op | source)
XLA Modules:
  0.0 145.9 jit_solution(5670462188865228826)
XLA Ops:
  0.6 0.7 convert_bitcast_fusion
  1.3 0.6 pad.4.places
  1.9 29.9 %shard_map.75 = (f32[256,256]{1,0:T(8,128)}, bf16[32,128,256]{2,1,0:T(8,128)(2,1)}, bf16[4,1040,128]{2,1,0:T(8,128)(2,1)}) custom-call(s32[1024,128]{1,0:T(8,128)} %bitcast.22, bf16[16,128]{1,0:T(8,128)(2,1)} %pad.4.places, f32[128,256]{1,0:T(8,128)} %current.1), custom_call_target="tpu_custom_call" | custom-call | tf_op jit(solution)/shard_map/pallas_call | solution.py:387
  31.8 1.3 slice.13
  33.1 0.7 slice_convert_fusion
  33.8 0.0 copy-start.1
  33.8 0.9 convert_reduce_fusion
  34.7 0.2 copy.16
  34.9 0.0 copy-start
  34.9 0.5 copy-done.1
  35.4 1.2 convolution_bitcast_fusion.coupled
  36.6 0.7 copy.18.degree.stats
  37.3 17.1 %shard_map.76 = (f32[128,256]{1,0:T(8,128)}, f32[128,256]{1,0:T(8,128)}, f32[128,256]{1,0:T(8,128)}, bf16[128,256]{1,0:T(8,128)(2,1)}, f32[8,128]{1,0:T(8,128)}) custom-call(f32[256,256]{1,0:T(8,128)} %get-tuple-element.24.gram, f32[128,256]{1,0:T(8,128)} %convolution_bitcast_fusion.coupled, f32[128,1]{1,0:T(8,128)} %copy.18.degree.stats, ...), custom_call_target="tpu_custom_call" | custom-call | tf_op jit(solution)/shard_map/pallas_call | solution.py:431
  54.4 0.0 copy-done
  54.4 20.4 %shard_map.77 = (f32[256,256]{1,0:T(8,128)}, f32[128,256]{1,0:T(8,128)}) custom-call(bf16[128,256]{1,0:T(8,128)(2,1)} %get-tuple-element.27.packed, bf16[32,128,128]{2,1,0:T(8,128)(2,1)} %bitcast.19), custom_call_target="tpu_custom_call" | custom-call | tf_op jit(solution)/shard_map/pallas_call | solution.py:430
  74.8 17.2 %shard_map.78 = (f32[128,256]{1,0:T(8,128)}, f32[128,256]{1,0:T(8,128)}, f32[128,256]{1,0:T(8,128)}, bf16[128,256]{1,0:T(8,128)(2,1)}, f32[8,128]{1,0:T(8,128)}) custom-call(f32[256,256]{1,0:T(8,128)} %get-tuple-element.28.gram, f32[128,256]{1,0:T(8,128)} %get-tuple-element.29.coupled, f32[128,1]{1,0:T(8,128)} %copy.18.degree.stats, ...), custom_call_target="tpu_custom_call" | custom-call | tf_op jit(solution)/shard_map/pallas_call | solution.py:431
  92.0 23.2 %shard_map.79 = (f32[256,256]{1,0:T(8,128)}, f32[128,256]{1,0:T(8,128)}) custom-call(bf16[128,256]{1,0:T(8,128)(2,1)} %get-tuple-element.34.packed, bf16[32,128,128]{2,1,0:T(8,128)(2,1)} %bitcast.20), custom_call_target="tpu_custom_call" | custom-call | tf_op jit(solution)/shard_map/pallas_call | solution.py:430
  115.2 17.0 %shard_map.80 = (f32[128,256]{1,0:T(8,128)}, f32[128,256]{1,0:T(8,128)}, f32[128,256]{1,0:T(8,128)}, bf16[128,256]{1,0:T(8,128)(2,1)}, f32[8,128]{1,0:T(8,128)}) custom-call(f32[256,256]{1,0:T(8,128)} %get-tuple-element.35.gram, f32[128,256]{1,0:T(8,128)} %get-tuple-element.36.coupled, f32[128,1]{1,0:T(8,128)} %copy.18.degree.stats, ...), custom_call_target="tpu_custom_call" | custom-call | tf_op jit(solution)/shard_map/pallas_call | solution.py:431
  132.2 12.3 %shard_map.81 = f32[8,128]{1,0:T(8,128)} custom-call(f32[8,128]{1,0:T(8,128)} %get-tuple-element.43.source), custom_call_target="tpu_custom_call" | custom-call | tf_op jit(solution)/shard_map/pallas_call | solution.py:441
  144.5 1.5 %multiply_reduce_fusion = (f32[3]{0:T(128)}, f32[3]{0:T(128)}) fusion(f32[8,128]{1,0:T(8,128)} %shard_map.81), kind=kLoop, calls=%fused_computation.8 | loop fusion | flops 6 | bytes 48 | tf_op jit(solution)/shard_map/div | solution.py:451
  (1 shorter events, 0.0 us)
Async XLA Ops:
  33.8 1.6 %copy-start.1 = (bf16[32,128,256]{2,1,0:T(8,128)(2,1)S(1)}, bf16[32,128,256]{2,1,0:T(8,128)(2,1)}, u32[]{:S(2)}) copy-start(bf16[32,128,256]{2,1,0:T(8,128)(2,1)} %get-tuple-element.26) | copy-start | bytes 6291460
  34.9 19.4 %copy-start = (bf16[4,8,128,128]{3,2,1,0:T(8,128)(2,1)}, bf16[4,8,128,128]{3,2,1,0:T(8,128)(2,1)S(1)}, u32[]{:S(2)}) copy-start(bf16[4,8,128,128]{3,2,1,0:T(8,128)(2,1)S(1)} %copy.16) | copy-start | bytes 3145732
